TPU v7x, 32 devices: a whole 2x2x4 slice. The times are simulated.
32 devices in a mesh: gx: 4 (over y, x), gy: 8 (over z, core).
Axes of the slice: x: 2, y: 2, z: 4, core: 2. Of those that a mesh axis runs over, the one named last changes fastest.
Arguments:
- density_one: float32 [512, 512, 512], P('gx', 'gy'), may hold values from -6 to 6
- density_two: float32 [512, 512, 512], P('gx', 'gy'), may hold values from -6 to 6
Outputs:
- correlation: float32 [512, 512, 512], P('gx', 'gy')
All inputs are finite; a program needn't handle non-finite values.
Results may differ from a plain program's by a relative error of at most 0.00013.
Values sent between devices are 32-bit elements; how exact they have to be, the bound alone decides.
No kernel may reach another device: no remote copies, remote signals or barrier semaphores. Data moves between devices by JAX's collectives and lax.ppermute only.
A program may use at most 256 MiB of HBM per device.

v0:
```python
import math

import jax
import jax.numpy as jnp
from jax import lax
from jax.sharding import PartitionSpec as P

exact_mode = lax.Precision.HIGHEST


def phases(numerator, denominator):
    radians = (numerator % denominator).astype(jnp.float32) * (2.0 * math.pi / denominator)
    return (jnp.cos(radians), jnp.sin(radians))


def complex_table(length, direction):
    positions = jnp.arange(length, dtype=jnp.int32)
    cosines, sines_raw = phases(positions[:, None] * positions[None, :], length)
    signed = direction * sines_raw
    real_rows = jnp.stack([cosines, signed], axis=1)
    imag_rows = jnp.stack([-signed, cosines], axis=1)
    return jnp.stack([real_rows, imag_rows], axis=0)


def depth_tables(depth_cells, count_x, count_y):
    half_depth = depth_cells // 2
    kz_slices = half_depth // (count_x * count_y)
    row_ids = jnp.arange(2 * half_depth, dtype=jnp.int32)
    within = row_ids % kz_slices
    imag_flag = row_ids // kz_slices % 2
    row_block = row_ids // (2 * kz_slices)
    row_block = row_block % count_y * count_x + row_block // count_y
    wave_number = row_block * kz_slices + within
    cell_ids = jnp.arange(depth_cells, dtype=jnp.int32)
    cosines, sines_raw = phases(wave_number[:, None] * cell_ids[None, :], depth_cells)
    is_imag = (imag_flag == 1)[:, None]
    forward = jnp.where(is_imag, -sines_raw, cosines)
    weight = jnp.where(wave_number == 0, 1.0, 2.0)[:, None]
    inverse = jnp.where(is_imag, -weight * sines_raw, weight * cosines)
    return (forward, inverse)


def on_device(density_one, density_two):
    count_x = lax.axis_size("gx")
    count_y = lax.axis_size("gy")
    x_local, y_local, depth_cells = density_one.shape
    grid_x = x_local * count_x
    grid_y = y_local * count_y
    kz_slices = depth_cells // 2 // (count_x * count_y)
    columns = x_local * y_local
    cell_total = float(grid_x * grid_y * depth_cells)
    forward_depth, inverse_depth = depth_tables(depth_cells, count_x, count_y)

    def depth_forward(density):
        flat_lines = density.reshape(columns, depth_cells)
        return lax.dot_general(
            forward_depth, flat_lines, (((1,), (1,)), ((), ())), precision=exact_mode
        )

    spectra = jnp.stack([depth_forward(density_one), depth_forward(density_two)])
    y_forward = complex_table(grid_y, -1.0).reshape(2, count_y, y_local, 2, grid_y)
    y_inverse = complex_table(grid_y, 1.0).reshape(2, grid_y, 2, count_y, y_local)
    block_forward = complex_table(count_x, -1.0)
    block_inverse = complex_table(count_x, 1.0)
    local_forward = complex_table(x_local, -1.0)
    sent = spectra.reshape(2, count_x * count_y, 2 * kz_slices, columns)
    moved = lax.all_to_all(sent, ("gx", "gy"), split_axis=1, concat_axis=1, tiled=True)
    moved = moved.reshape(2, count_x, count_y, 2, kz_slices, x_local, y_local)
    planes = jnp.einsum("fdspkjy,psyrq->fdrkjq", moved, y_forward, precision=exact_mode)
    aligned = jnp.einsum("fdpkjq,pdra->farkjq", planes, block_forward, precision=exact_mode)
    twiddle_cos, twiddle_sin = phases(
        jnp.arange(count_x, dtype=jnp.int32)[:, None]
        * jnp.arange(x_local, dtype=jnp.int32)[None, :],
        grid_x,
    )
    forward_cos = twiddle_cos[None, :, None, :, None]
    forward_sin = twiddle_sin[None, :, None, :, None]
    real_part = aligned[:, :, 0]
    imag_part = aligned[:, :, 1]
    turned = jnp.stack(
        [
            real_part * forward_cos + imag_part * forward_sin,
            imag_part * forward_cos - real_part * forward_sin,
        ],
        axis=2,
    )
    spectra_k = jnp.einsum("fapkjq,pjrb->farkbq", turned, local_forward, precision=exact_mode)
    power = (
        spectra_k[0, :, 0] * spectra_k[1, :, 0] + spectra_k[0, :, 1] * spectra_k[1, :, 1]
    ) / cell_total
    wave_x = (
        jnp.arange(count_x, dtype=jnp.int32)[:, None]
        + count_x * jnp.arange(x_local, dtype=jnp.int32)[None, :]
    )
    keep_x = (wave_x != grid_x // 2)[:, None, :, None]
    keep_y = (jnp.arange(grid_y, dtype=jnp.int32) != grid_y // 2)[None, None, None, :]
    power = jnp.where(keep_x & keep_y, power, 0.0)
    cos_local, sin_local = phases(
        jnp.arange(x_local, dtype=jnp.int32)[:, None]
        * jnp.arange(x_local, dtype=jnp.int32)[None, :],
        x_local,
    )
    real_table = jnp.stack([cos_local, sin_local], axis=1)
    lines = jnp.einsum("akbq,brj->arkjq", power, real_table, precision=exact_mode)
    inverse_cos = twiddle_cos[:, None, :, None]
    inverse_sin = twiddle_sin[:, None, :, None]
    real_part = lines[:, 0]
    imag_part = lines[:, 1]
    unturned = jnp.stack(
        [
            real_part * inverse_cos - imag_part * inverse_sin,
            imag_part * inverse_cos + real_part * inverse_sin,
        ],
        axis=1,
    )[None]
    blocks = jnp.einsum("fapkjq,pard->fdrkjq", unturned, block_inverse, precision=exact_mode)
    back_lines = jnp.einsum("fdpkjq,pqrsy->fdsrkjy", blocks, y_inverse, precision=exact_mode)
    sent_back = back_lines.reshape(1, count_x * count_y, 2 * kz_slices, columns)
    rows_back = lax.all_to_all(sent_back, ("gx", "gy"), split_axis=1, concat_axis=1, tiled=True)
    rows_flat = rows_back.reshape(2 * kz_slices * count_x * count_y, columns)
    correlation = lax.dot_general(
        rows_flat, inverse_depth, (((0,), (0,)), ((), ())), precision=exact_mode
    )
    correlation = correlation * (1.0 / math.sqrt(cell_total))
    return correlation.reshape(x_local, y_local, depth_cells)


def solution(mesh):
    return jax.shard_map(
        on_device,
        mesh=mesh,
        in_specs=(P("gx", "gy", None), P("gx", "gy", None)),
        out_specs=P("gx", "gy", None),
        check_vma=False,
    )
```

profile of v0, /device:TPU:0, one launch (start us, length us, event | category | flops | bytes accessed | tf_op | source)
XLA Modules:
  0.0 2118.7 jit_solution(7374333647486353023)
XLA Ops:
  0.1 0.0 slice-start
  0.1 4.3 fusion.212
  4.4 4.3 fusion.214
  8.7 0.0 slice-start.1
  8.7 32.4 %convolution_bitcast_fusion = f32[1,32,16,8192]{3,2,1,0:T(8,128)} fusion(f32[8192,512,1]{1,0,2:T(8,128)} %bitcast.172, f32[32,16,512]{2,1,0:T(8,128)S(1)} %fusion.212), kind=kOutput, calls=%fused_computation.18 | convolution fusion | flops 25769803776 | bytes 34603008 | tf_op jit(solution)/shard_map/dot_general | solution.py:56
  41.2 29.7 %convolution_bitcast_fusion.1 = f32[1,32,16,8192]{3,2,1,0:T(8,128)} fusion(f32[8192,512,1]{1,0,2:T(8,128)S(1)} %bitcast.175, f32[32,16,512]{2,1,0:T(8,128)S(1)} %fusion.214), kind=kOutput, calls=%fused_computation.19 | convolution fusion | flops 25769803776 | bytes 34603008 | tf_op jit(solution)/shard_map/dot_general | solution.py:56
  70.8 12.4 pad_maximum_fusion
  83.3 11.1 copy.45
  94.3 7.7 all-to-all-start
  102.0 0.1 fusion.171
  102.1 0.1 fusion.168
  102.1 0.1 broadcast_multiply_fusion.1
  102.2 0.1 copy.44
  102.3 0.1 copy.43
  102.4 0.1 fusion.165
  102.5 0.1 copy.50
  102.6 0.4 copy-done.9
  103.0 0.1 copy.49
  103.1 0.7 copy.41
  103.8 0.7 copy.40
  104.5 0.3 fusion.115
  104.8 0.9 fusion.113
  105.7 0.3 broadcast_multiply_fusion
  106.0 0.6 copy-done.4
  106.6 0.7 fusion.105
  107.3 4.2 sine_multiply_fusion
  111.5 2.6 maximum_bitcast_fusion.21
  114.1 0.9 broadcast_and_fusion
  115.0 6.0 fusion.96
  121.0 705.1 %all-to-all-done = f32[2,32,16,8192]{3,2,0,1:T(8,128)} async-done(((f32[2,32,16,8192]{3,2,0,1:T(8,128)}), f32[2,32,16,8192]{3,2,0,1:T(8,128)}, u32[]{:S(2)}, u32[]{:S(2)}) %all-to-all-start) | async-done | bytes 33554464 | tf_op jit(solution)/shard_map/all_to_all | solution.py:67
  826.1 52.6 %reshape.673 = f32[2,4,8,2,8,128,64]{6,5,4,3,0,2,1:T(8,128)} reshape(f32[2,32,16,8192]{3,2,0,1:T(8,128)} %all-to-all-done) | data formatting | bytes 67108864 | tf_op jit(solution)/shard_map/reshape | solution.py:68
  878.7 433.2 %fusion.18 = f32[2,4,2,8,128,512]{4,5,3,1,0,2:T(8,128)} fusion(f32[2,4,8,2,8,128,64]{6,5,4,3,0,2,1:T(8,128)} %reshape.673, f32[2,8,64,2,512,1,1,1]{4,2,1,0,7,6,5,3:T(8,128)} %maximum_bitcast_fusion.21), kind=kOutput, calls=%fused_computation.21 | convolution fusion | flops 103079215104 | bytes 71303168 | tf_op jit(solution)/shard_map/fdspkjy,psyrq->fdrkjq/dot_general | solution.py:69
  1311.9 39.3 %copy.48 = f32[2,4,2,8,128,512]{5,1,2,4,3,0:T(4,128)} copy(f32[2,4,2,8,128,512]{4,5,3,1,0,2:T(8,128)} %fusion.18) | data formatting | bytes 67108864 | tf_op jit(solution)/shard_map/fdspkjy,psyrq->fdrkjq/transpose | solution.py:69
  1351.1 74.9 %fusion.7 = f32[2,4,2,8,128,512]{5,1,4,3,0,2:T(4,128)} fusion(f32[2,4,2,8,128,512]{5,1,2,4,3,0:T(4,128)} %copy.48, f32[2,4,2,4,1,1,1]{1,3,0,6,5,4,2:T(4,128)S(1)} %maximum_bitcast_fusion.20), kind=kOutput, calls=%fused_computation.9 | convolution fusion | flops 805306368 | bytes 67109120 | tf_op jit(solution)/shard_map/fdpkjq,pdra->farkjq/dot_general | solution.py:70
  1426.0 27.3 %multiply_add_fusion = (f32[2,4,1,8,128,512]{5,1,4,3,0,2:T(4,128)}, f32[2,4,1,8,128,512]{5,1,4,3,0,2:T(4,128)}) fusion(f32[2,4,2,8,128,512]{5,1,4,3,0,2:T(4,128)} %fusion.7, f32[4,128]{0,1:T(8,128)S(1)} %copy.50, f32[4,128]{0,1:T(8,128)S(1)} %copy.49), kind=kLoop, calls=%fused_computation.17 | loop fusion | flops 25165824 | bytes 67112960 | tf_op jit(solution)/shard_map/add | solution.py:82
  1453.3 23.0 %pad_maximum_fusion.1 = f32[2,4,2,8,128,512]{5,1,4,3,0,2:T(4,128)} fusion(f32[2,4,1,8,128,512]{5,1,4,3,0,2:T(4,128)} %get-tuple-element.6, f32[2,4,1,8,128,512]{5,1,4,3,0,2:T(4,128)} %get-tuple-element.5), kind=kLoop, calls=%fused_computation.3 | loop fusion | flops 8388608 | bytes 67108864 | tf_op jit(solution)/shard_map/stack | solution.py:80
  1476.3 45.4 %fusion.15 = f32[2,4,2,8,128,512]{5,4,3,1,0,2:T(8,128)} fusion(f32[2,4,2,8,128,512]{5,1,4,3,0,2:T(4,128)} %pad_maximum_fusion.1, f32[1,128,2,128]{1,3,0,2:T(8,128)S(1)} %copy-done.7, f32[1,128,2,128]{1,3,0,2:T(8,128)S(1)} %copy-done.6), kind=kOutput, calls=%fused_computation.20 | convolution fusion | flops 25769869312 | bytes 67371008 | tf_op jit(solution)/shard_map/fapkjq,pjrb->farkbq/dot_general | solution.py:87
  1521.8 23.0 %fusion.33 = f32[4,2,8,128,512]{4,3,2,0,1:T(8,128)} fusion(f32[2,4,2,8,128,512]{5,4,3,1,0,2:T(8,128)} %fusion.15, pred[4,128,512]{2,1,0:T(8,128)(4,1)S(1)} %copy-done, f32[128,1,128]{0,2,1:T(8,128)S(1)} %copy-done.5, f32[128,1,128]{0,2,1:T(8,128)S(1)} %copy-done.8), kind=kOutput, calls=%fused_computation.36 | convolution fusion | flops 6452969472 | bytes 50724864 | tf_op jit(solution)/shard_map/akbq,brj->arkjq/dot_general | solution.py:104
  1544.8 11.0 multiply_subtract_fusion.1
  1555.8 6.9 pad_maximum_fusion.2
  1562.8 44.0 %fusion.21 = f32[4,2,8,128,512,1,1]{4,0,3,2,1,6,5:T(4,128)} fusion(f32[4,2,8,128,512]{4,3,2,0,1:T(8,128)S(1)} %pad_maximum_fusion.2, f32[1,4,2,4]{1,3,0,2:T(4,128)S(1)} %copy-done.13, f32[1,4,2,4]{1,3,0,2:T(4,128)S(1)} %copy-done.14), kind=kOutput, calls=%fused_computation.23 | convolution fusion | flops 402653248 | bytes 33554688 | tf_op jit(solution)/shard_map/fapkjq,pard->fdrkjq/dot_general | solution.py:116
  1606.8 60.9 %fusion.36 = f32[1,4,8,2,8,128,64]{5,6,4,1,2,3,0:T(8,128)} fusion(f32[4,2,8,128,512,1,1]{4,0,3,2,1,6,5:T(4,128)} %fusion.21, f32[1,512,1,8,64]{1,4,0,3,2:T(8,128)S(1)} %copy-done.3, f32[1,512,1,8,64]{1,4,0,3,2:T(8,128)S(1)} %copy-done.2, f32[1,512,1,8,64]{1,4,0,3,2:T(8,128)S(1)} %copy-done.1), kind=kOutput, calls=%fused_computation.37 | convolution fusion | flops 51542753280 | bytes 36700160 | tf_op jit(solution)/shard_map/fdpkjq,pqrsy->fdsrkjy/dot_general | solution.py:117
  1667.7 23.0 %copy.54 = f32[1,4,8,2,8,128,64]{6,5,4,3,2,1,0:T(8,128)} copy(f32[1,4,8,2,8,128,64]{5,6,4,1,2,3,0:T(8,128)} %fusion.36) | data formatting | bytes 33554432 | tf_op jit(solution)/shard_map/fdpkjq,pqrsy->fdsrkjy/transpose | solution.py:117
  1690.8 27.9 %reshape.651 = f32[1,32,16,8192]{3,2,1,0:T(8,128)} reshape(f32[1,4,8,2,8,128,64]{6,5,4,3,2,1,0:T(8,128)} %copy.54) | data formatting | bytes 33554432 | tf_op jit(solution)/shard_map/reshape | solution.py:118
  1718.7 3.9 all-to-all-start.1
  1722.6 4.4 fusion.217
  1727.0 360.1 %all-to-all-done.1 = f32[1,32,16,8192]{3,2,0,1:T(8,128)} async-done(((f32[1,32,16,8192]{3,2,0,1:T(8,128)}), f32[1,32,16,8192]{3,2,0,1:T(8,128)}, u32[]{:S(2)}, u32[]{:S(2)}) %all-to-all-start.1) | async-done | bytes 16777248 | tf_op jit(solution)/shard_map/all_to_all | solution.py:119
  2087.1 31.2 %convolution_multiply_fusion = f32[8192,512]{1,0:T(8,128)} fusion(f32[512,8192]{1,0:T(8,128)} %bitcast.55, f32[512,512]{1,0:T(8,128)S(1)} %fusion.217), kind=kOutput, calls=%fused_computation.22 | convolution fusion | flops 25773998080 | bytes 34603008 | tf_op jit(solution)/shard_map/dot_general | solution.py:121
  (46 shorter events, 0.2 us)
Async XLA Ops:
  0.1 41.1 %slice-start = ((s8[16777216]{0:T(1024)(128)(4,1)}), s8[4194304]{0:T(1024)(128)(4,1)S(1)}, s32[]{:S(2)}) async-start(s8[16777216]{0:T(1024)(128)(4,1)} %bitcast.173), calls=%async_computation.2 | async-start | bytes 8388608
  8.7 32.5 %slice-start.1 = ((s8[16777216]{0:T(1024)(128)(4,1)}), s8[4194304]{0:T(1024)(128)(4,1)S(1)}, s32[]{:S(2)}) async-start(s8[16777216]{0:T(1024)(128)(4,1)} %bitcast.173), calls=%async_computation.3 | async-start | bytes 8388608
  8.7 32.4 %slice-start.2 = ((s8[16777216]{0:T(1024)(128)(4,1)}), s8[4194304]{0:T(1024)(128)(4,1)S(1)}, s32[]{:S(2)}) async-start(s8[16777216]{0:T(1024)(128)(4,1)} %bitcast.173), calls=%async_computation.4 | async-start | bytes 8388608
  8.7 32.4 %slice-start.3 = ((s8[16777216]{0:T(1024)(128)(4,1)}), s8[4194304]{0:T(1024)(128)(4,1)S(1)}, s32[]{:S(2)}) async-start(s8[16777216]{0:T(1024)(128)(4,1)} %bitcast.173), calls=%async_computation.5 | async-start | bytes 8388608
  94.3 731.7 %all-to-all-start = ((f32[2,32,16,8192]{3,2,0,1:T(8,128)}), f32[2,32,16,8192]{3,2,0,1:T(8,128)}, u32[]{:S(2)}, u32[]{:S(2)}) async-start(f32[2,32,16,8192]{3,2,0,1:T(8,128)} %copy.45), calls=%async_computation | async-start | bytes 67108864 | tf_op jit(solution)/shard_map/all_to_all | solution.py:67
  102.5 0.5 copy-start.9
  102.5 2.0 copy-start.11
  106.0 0.6 copy-start.4
  1453.3 23.0 %copy-start.6 = (f32[1,128,2,128]{1,3,0,2:T(8,128)S(1)}, f32[1,128,2,128]{1,3,0,2:T(8,128)}, u32[]{:S(2)}) copy-start(f32[1,128,2,128]{1,3,0,2:T(8,128)} %get-tuple-element.9) | copy-start | bytes 393220
  1453.3 23.0 %copy-start.7 = (f32[1,128,2,128]{1,3,0,2:T(8,128)S(1)}, f32[1,128,2,128]{1,3,0,2:T(8,128)}, u32[]{:S(2)}) copy-start(f32[1,128,2,128]{1,3,0,2:T(8,128)} %get-tuple-element.10) | copy-start | bytes 393220
  1476.3 45.5 %copy-start = (pred[4,128,512]{2,1,0:T(8,128)(4,1)S(1)}, pred[4,128,512]{2,1,0:T(8,128)(4,1)}, u32[]{:S(2)}) copy-start(pred[4,128,512]{2,1,0:T(8,128)(4,1)} %broadcast_and_fusion) | copy-start | bytes 786436
  1476.3 45.5 %copy-start.5 = (f32[128,1,128]{0,2,1:T(8,128)S(1)}, f32[128,1,128]{0,2,1:T(8,128)}, u32[]{:S(2)}) copy-start(f32[128,1,128]{0,2,1:T(8,128)} %copy-done.4) | copy-start | bytes 196612
  1476.3 45.5 %copy-start.8 = (f32[128,1,128]{0,2,1:T(8,128)S(1)}, f32[128,1,128]{0,2,1:T(8,128)}, u32[]{:S(2)}) copy-start(f32[128,1,128]{0,2,1:T(8,128)} %fusion.113) | copy-start | bytes 196612
  1521.8 23.1 %copy-start.10 = (f32[4,128]{1,0:T(4,128)S(1)}, f32[4,128]{1,0:T(4,128)}, u32[]{:S(2)}) copy-start(f32[4,128]{1,0:T(4,128)} %copy-done.9) | copy-start | bytes 6148
  1521.8 23.1 %copy-start.12 = (f32[4,128]{1,0:T(4,128)S(1)}, f32[4,128]{1,0:T(4,128)}, u32[]{:S(2)}) copy-start(f32[4,128]{1,0:T(4,128)} %copy-done.11) | copy-start | bytes 6148
  1555.8 6.9 copy-start.13
  1555.8 7.0 copy-start.14
  1562.8 44.0 %copy-start.1 = (f32[1,512,1,8,64]{1,4,0,3,2:T(8,128)S(1)}, f32[1,512,1,8,64]{1,4,0,3,2:T(8,128)}, u32[]{:S(2)}) copy-start(f32[1,512,1,8,64]{1,4,0,3,2:T(8,128)} %get-tuple-element.11) | copy-start | bytes 3145732
  1562.8 44.0 %copy-start.2 = (f32[1,512,1,8,64]{1,4,0,3,2:T(8,128)S(1)}, f32[1,512,1,8,64]{1,4,0,3,2:T(8,128)}, u32[]{:S(2)}) copy-start(f32[1,512,1,8,64]{1,4,0,3,2:T(8,128)} %get-tuple-element.12) | copy-start | bytes 3145732
  1562.8 44.0 %copy-start.3 = (f32[1,512,1,8,64]{1,4,0,3,2:T(8,128)S(1)}, f32[1,512,1,8,64]{1,4,0,3,2:T(8,128)}, u32[]{:S(2)}) copy-start(f32[1,512,1,8,64]{1,4,0,3,2:T(8,128)} %get-tuple-element.13) | copy-start | bytes 3145732
  1718.7 368.4 %all-to-all-start.1 = ((f32[1,32,16,8192]{3,2,0,1:T(8,128)}), f32[1,32,16,8192]{3,2,0,1:T(8,128)}, u32[]{:S(2)}, u32[]{:S(2)}) async-start(f32[1,32,16,8192]{3,2,0,1:T(8,128)} %bitcast.171), calls=%async_computation.1 | async-start | bytes 33554432 | tf_op jit(solution)/shard_map/all_to_all | solution.py:119
where the time goes:
time: 2130 us; the launch traced here: 2120 us
  waiting for transfers between devices  1070 us (50%)
  matrix products  775 us (36%)
  local copies, waits for them, and re-layouts  157 us (7%)
  other arithmetic  110 us (5%)
    all_to_all x1, waiting for transfers between devices, on_device(): lax.all_to_all(sent, ('gx', 'gy'), split_axis=1, concat_axis=1, tiled=True)  705 us
    dot_general x1, matrix products, on_device(): jnp.einsum('fdspkjy,psyrq->fdrkjq', moved, y_forward, precision=exact_mode)  433 us
    all_to_all x1, waiting for transfers between devices, on_device(): lax.all_to_all(sent_back, ('gx', 'gy'), split_axis=1, concat_axis=1, tile...  360 us
    dot_general x1, matrix products, on_device(): jnp.einsum('fdpkjq,pdra->farkjq', planes, block_forward, precision=exact_...  74.9 us
    dot_general x2, matrix products, depth_forward(): lax.dot_general(forward_depth, flat_lines, (((1,), (1,)), ((), ())), prec...  62.1 us
    dot_general x1, matrix products, on_device(): jnp.einsum('fdpkjq,pqrsy->fdsrkjy', blocks, y_inverse, precision=exact_mode)  60.9 us
    reshape x1, local copies, waits for them, and re-layouts, on_device(): moved = moved.reshape(2, count_x, count_y, 2, kz_slices, x_local, y_local)  52.6 us
    dot_general x1, matrix products, on_device(): jnp.einsum('fapkjq,pjrb->farkbq', turned, local_forward, precision=exact_...  45.4 us
  transfers between devices with their start and end apart: 2, of which 2 were waited for; matrix products, arithmetic and copies ran while one was open for 1% of the time, Pallas kernels for 0%

commit v1 on v0

--- a/solution.py
+++ b/solution.py
@@ -3,6 +3,8 @@
 import jax
 import jax.numpy as jnp
 from jax import lax
+from jax.experimental import pallas as pl
+from jax.experimental.pallas import tpu as pltpu
 from jax.sharding import PartitionSpec as P
 
 exact_mode = lax.Precision.HIGHEST
@@ -40,7 +42,7 @@
     return (forward, inverse)
 
 
-def on_device(density_one, density_two):
+def generic_device(density_one, density_two):
     count_x = lax.axis_size("gx")
     count_y = lax.axis_size("gy")
     x_local, y_local, depth_cells = density_one.shape
@@ -125,6 +127,316 @@
     return correlation.reshape(x_local, y_local, depth_cells)
 
 
+VMEM_LIMIT = 60 * 1024 * 1024
+MAX_CHUNKS = 2
+Y_BLOCK = 8
+
+
+def split(value):
+    high = value.astype(jnp.bfloat16)
+    low = (value - high.astype(jnp.float32)).astype(jnp.bfloat16)
+    return high, low
+
+
+def dot3(left_high, left_low, right_high, right_low):
+    def one(a, b):
+        return jnp.dot(a, b, preferred_element_type=jnp.float32)
+
+    return one(left_high, right_high) + one(left_high, right_low) + one(left_low, right_high)
+
+
+def cosine_pair(steps, length, factor=None):
+    turned = jnp.cos((steps % length).astype(jnp.float32) * (2.0 * math.pi / length))
+    if factor is not None:
+        turned = turned * factor
+    high = lax.reduce_precision(turned, 8, 7)
+    return high.astype(jnp.bfloat16), (turned - high).astype(jnp.bfloat16)
+
+
+def depth_rows(chunk, chunks, devices, kz_slices):
+    per_chunk = kz_slices // chunks
+    rows = jnp.arange(devices * 2 * per_chunk, dtype=jnp.int32)
+    device = rows // (2 * per_chunk)
+    flag = rows // per_chunk % 2
+    return device * kz_slices + chunk * per_chunk + rows % per_chunk, flag
+
+
+def depth_forward_kernel(one_ref, two_ref, high_ref, low_ref, out_ref, turn_ref):
+    x_local, y_block, depth = one_ref.shape
+    rows = high_ref.shape[1]
+    lines = x_local * y_block
+    step = min(256, lines)
+    group = out_ref.shape[2] * out_ref.shape[3]
+    flat_out = out_ref.reshape(2 * rows * y_block, x_local)
+    for field, ref in enumerate((one_ref, two_ref)):
+        flat = ref.reshape(lines, depth)
+
+        def multiply(i, carry):
+            high, low = split(flat[pl.ds(i * step, step), :])
+            product = dot3(high, low, high_ref[...], low_ref[...])
+            for part in range(rows // 128):
+                turn_ref[field, part, pl.ds(i * step, step), :] = product[:, part * 128 : part * 128 + 128]
+            return carry
+
+        lax.fori_loop(0, lines // step, multiply, 0)
+    for field in range(2):
+        for part in range(rows // 128):
+            lanes = turn_ref.at[field, part]
+            for j in range(y_block):
+                block = lanes[pl.ds(j, x_local, stride=y_block), :]
+                turned = block.T
+                for d in range(128 // group):
+                    start = (2 * (part * (128 // group) + d) + field) * group * y_block + j
+                    flat_out[pl.ds(start, group, stride=y_block), :] = turned[d * group : d * group + group]
+
+
+def depth_forward(one, two, table, rows_shape):
+    x_local, y_local, depth = one.shape
+    rows = math.prod(rows_shape)
+    out_rows = (rows_shape[0], 2, *rows_shape[1:])
+    field_spec = pl.BlockSpec((x_local, Y_BLOCK, depth), lambda i: (0, i, 0))
+    table_spec = pl.BlockSpec((depth, rows), lambda i: (0, 0))
+    return pl.pallas_call(
+        depth_forward_kernel,
+        grid=(y_local // Y_BLOCK,),
+        in_specs=[field_spec, field_spec, table_spec, table_spec],
+        out_specs=pl.BlockSpec((*out_rows, Y_BLOCK, x_local), lambda i: (0, 0, 0, 0, i, 0)),
+        out_shape=jax.ShapeDtypeStruct((*out_rows, y_local, x_local), jnp.float32),
+        scratch_shapes=[pltpu.VMEM((2, rows // 128, x_local * Y_BLOCK, 128), jnp.float32)],
+        compiler_params=pltpu.CompilerParams(vmem_limit_bytes=VMEM_LIMIT),
+        name="depth_forward",
+    )(one, two, *table)
+
+
+def depth_inverse_kernel(*refs):
+    *part_refs, high_ref, low_ref, out_ref, turn_ref = refs
+    x_local, y_block, depth = out_ref.shape
+    lines = x_local * y_block
+    blocks = 0
+    for part_ref in part_refs:
+        rows = part_ref.shape[0] * part_ref.shape[1] * part_ref.shape[2]
+        flat = part_ref.reshape(rows * y_block, x_local)
+        for part in range(rows // 128):
+            for j in range(y_block):
+                block = flat[pl.ds(part * 128 * y_block + j, 128, stride=y_block), :]
+                turn_ref[blocks, pl.ds(j, x_local, stride=y_block), :] = block.T
+            blocks += 1
+    step = min(256, lines)
+    flat_out = out_ref.reshape(lines, depth)
+
+    def multiply(i, carry):
+        window = pl.ds(i * step, step)
+        left = jnp.concatenate([turn_ref[b, window, :] for b in range(blocks)], axis=1)
+        high, low = split(left)
+        flat_out[window, :] = dot3(high, low, high_ref[...], low_ref[...])
+        return carry
+
+    lax.fori_loop(0, lines // step, multiply, 0)
+
+
+def depth_inverse(parts, table):
+    devices, two, kz_chunk, y_local, x_local = parts[0].shape
+    rows, depth = table[0].shape
+    part_spec = pl.BlockSpec((devices, two, kz_chunk, Y_BLOCK, x_local), lambda i: (0, 0, 0, i, 0))
+    table_spec = pl.BlockSpec((rows, depth), lambda i: (0, 0))
+    return pl.pallas_call(
+        depth_inverse_kernel,
+        grid=(y_local // Y_BLOCK,),
+        in_specs=[part_spec] * len(parts) + [table_spec, table_spec],
+        out_specs=pl.BlockSpec((x_local, Y_BLOCK, depth), lambda i: (0, i, 0)),
+        out_shape=jax.ShapeDtypeStruct((x_local, y_local, depth), jnp.float32),
+        scratch_shapes=[pltpu.VMEM((rows // 128, x_local * Y_BLOCK, 128), jnp.float32)],
+        compiler_params=pltpu.CompilerParams(vmem_limit_bytes=VMEM_LIMIT),
+        name="depth_inverse",
+    )(*parts, *table)
+
+
+def plane_kernel(
+    s_ref, wy_high, wy_low, wx_high, wx_low, vx_high, vx_low, vy_high, vy_low, out_ref,
+    s_high, s_low, y_high, y_low, p_high, p_low, g_high, g_low, *, count_x, count_y, tile, scale,
+):
+    y_local, x_local = out_ref.shape[-2:]
+    grid_x, grid_y = count_x * x_local, count_y * y_local
+    pair = 2 * y_local
+
+    def load(i, carry):
+        field, row = i // count_y, i % count_y
+        for g in range(count_x):
+            values = s_ref[g * count_y + row, field].reshape(pair, x_local)
+            high, low = split(values)
+            here = (field, pl.ds(row * pair, pair), slice(g * x_local, (g + 1) * x_local))
+            s_high[here] = high
+            s_low[here] = low
+        return carry
+
+    lax.fori_loop(0, 2 * count_y, load, 0)
+
+    def middle(t, carry):
+        rows = pl.ds(t * 2 * tile, 2 * tile)
+        for field in range(2):
+            for b in range(grid_x // 256):
+                columns = slice(b * 256, b * 256 + 256)
+                planes = dot3(
+                    wy_high[rows, :], wy_low[rows, :], s_high[field, :, columns], s_low[field, :, columns]
+                )
+                high, low = split(planes)
+                for r in range(2):
+                    lanes = slice(r * grid_x + b * 256, r * grid_x + b * 256 + 256)
+                    y_high[field * tile : (field + 1) * tile, lanes] = high[r * tile : (r + 1) * tile]
+                    y_low[field * tile : (field + 1) * tile, lanes] = low[r * tile : (r + 1) * tile]
+        for b in range(grid_x // 256):
+            power = None
+            for r in range(2):
+                columns = slice(r * grid_x + b * 256, r * grid_x + b * 256 + 256)
+                z = dot3(y_high[...], y_low[...], wx_high[:, columns], wx_low[:, columns])
+                term = z[:tile] * z[tile:]
+                power = term if power is None else power + term
+            wave_y = t * tile + lax.broadcasted_iota(jnp.int32, power.shape, 0)
+            wave_x = b * 256 + lax.broadcasted_iota(jnp.int32, power.shape, 1)
+            keep = (wave_x != grid_x // 2) & (wave_y != grid_y // 2)
+            high, low = split(jnp.where(keep, power * scale, 0.0))
+            p_high[:, b * 256 : b * 256 + 256] = high
+            p_low[:, b * 256 : b * 256 + 256] = low
+        for r in range(2):
+            for b in range(grid_x // 256):
+                columns = slice(r * grid_x + b * 256, r * grid_x + b * 256 + 256)
+                lines = dot3(p_high[...], p_low[...], vx_high[:, columns], vx_low[:, columns])
+                high, low = split(lines)
+                here = (pl.ds(r * grid_y + t * tile, tile), slice(b * 256, b * 256 + 256))
+                g_high[here] = high
+                g_low[here] = low
+        return carry
+
+    lax.fori_loop(0, grid_y // tile, middle, 0)
+    per_step = min(count_y, max(1, 512 // pair))
+
+    def back(i, carry):
+        rows = pl.ds(i * per_step * pair, per_step * pair)
+        for b in range(grid_x // 256):
+            columns = slice(b * 256, b * 256 + 256)
+            result = dot3(vy_high[rows, :], vy_low[rows, :], g_high[:, columns], g_low[:, columns])
+            for h in range(256 // x_local):
+                g = b * (256 // x_local) + h
+                for j in range(per_step):
+                    piece = result[j * pair : (j + 1) * pair, h * x_local : (h + 1) * x_local]
+                    out_ref[g * count_y + i * per_step + j] = piece.reshape(2, 1, y_local, x_local)
+        return carry
+
+    lax.fori_loop(0, count_y // per_step, back, 0)
+
+
+def plane_tile(grid_y):
+    return min(256, grid_y)
+
+
+def planes(received, tables, count_x, count_y, scale):
+    devices, _, _, kz_chunk, y_local, x_local = received.shape
+    grid_x, grid_y = count_x * x_local, count_y * y_local
+    tile = plane_tile(grid_y)
+
+    def whole(array):
+        return pl.BlockSpec(array.shape, lambda i: (0, 0), pipeline_mode=pl.Buffered(1))
+
+    flat_tables = [part for pair in tables for part in pair]
+
+    def scratch(*shape):
+        return [pltpu.VMEM(shape, jnp.bfloat16)] * 2
+
+    def body(*refs):
+        plane_kernel(*refs, count_x=count_x, count_y=count_y, tile=tile, scale=scale)
+
+    return pl.pallas_call(
+        body,
+        grid=(kz_chunk,),
+        in_specs=[
+            pl.BlockSpec((devices, 2, 2, 1, y_local, x_local), lambda i: (0, 0, 0, i, 0, 0)),
+            *[whole(part) for part in flat_tables],
+        ],
+        out_specs=pl.BlockSpec((devices, 2, 1, y_local, x_local), lambda i: (0, 0, i, 0, 0)),
+        out_shape=jax.ShapeDtypeStruct((devices, 2, kz_chunk, y_local, x_local), jnp.float32),
+        scratch_shapes=[
+            *scratch(2, 2 * grid_y, grid_x),
+            *scratch(2 * tile, 2 * grid_x),
+            *scratch(tile, grid_x),
+            *scratch(2 * grid_y, grid_x),
+        ],
+        compiler_params=pltpu.CompilerParams(vmem_limit_bytes=VMEM_LIMIT),
+        name="planes",
+    )(received, *flat_tables)
+
+
+def plane_tables(anchor, grid_x, grid_y, count_y):
+    y_local = grid_y // count_y
+    tile = plane_tile(grid_y)
+
+    def ids(length):
+        return jnp.arange(length, dtype=jnp.int32) + anchor
+
+    inner = ids(2 * grid_y)
+    inner_y = inner // (2 * y_local) * y_local + inner % y_local
+    inner_r = inner // y_local % 2
+    outer_ky = inner // (2 * tile) * tile + inner % tile
+    outer_r = inner // tile % 2
+    wy = cosine_pair(
+        outer_ky[:, None] * inner_y[None, :] + (outer_r[:, None] - inner_r[None, :] + 4) * (grid_y // 4), grid_y
+    )
+    plain = ids(2 * grid_x)
+    plain_x, plain_r = plain % grid_x, plain // grid_x
+    wx = cosine_pair(
+        plain_x[:, None] * plain_x[None, :] + (plain_r[None, :] - plain_r[:, None] + 4) * (grid_x // 4), grid_x
+    )
+    vx = cosine_pair(ids(grid_x)[:, None] * plain_x[None, :] + (4 - plain_r[None, :]) * (grid_x // 4), grid_x)
+    wave_y, wave_r = inner % grid_y, inner // grid_y
+    vy = cosine_pair(
+        inner_y[:, None] * wave_y[None, :] + (wave_r[None, :] - inner_r[:, None] + 4) * (grid_y // 4), grid_y
+    )
+    return wy, wx, vx, vy
+
+
+def on_device(density_one, density_two):
+    count_x = lax.axis_size("gx")
+    count_y = lax.axis_size("gy")
+    x_local, y_local, depth = density_one.shape
+    grid_x, grid_y = x_local * count_x, y_local * count_y
+    devices = count_x * count_y
+    kz_slices = depth // 2 // devices
+    chunks = MAX_CHUNKS if kz_slices % MAX_CHUNKS == 0 else 1
+    kz_chunk = kz_slices // chunks
+    rows = devices * 2 * kz_chunk
+    fits = x_local % 128 == 0 and y_local % 8 == 0 and rows % 128 == 0 and 2 * kz_chunk % 8 == 0 and grid_x % 256 == 0 and grid_y % 256 == 0
+    if not fits:
+        return generic_device(density_one, density_two)
+    cell_total = float(grid_x * grid_y * depth)
+    cells = jnp.arange(depth, dtype=jnp.int32)
+    rows_shape = (devices, 2, kz_chunk)
+
+    def forward_table(chunk, anchor):
+        wave, flag = depth_rows(chunk, chunks, devices, kz_slices)
+        wave = wave + anchor
+        return cosine_pair(cells[:, None] * wave[None, :] + flag[None, :] * (depth // 4), depth)
+
+    def inverse_table(anchor):
+        waves, flags = zip(*(depth_rows(chunk, chunks, devices, kz_slices) for chunk in range(chunks)))
+        wave = jnp.concatenate(waves) + anchor
+        flag = jnp.concatenate(flags)
+        weight = jnp.where(wave == 0, 1.0, 2.0) * (1.0 / math.sqrt(cell_total))
+        return cosine_pair(wave[:, None] * cells[None, :] + flag[:, None] * (depth // 4), depth, weight[:, None])
+
+    zero = jnp.zeros((), jnp.int32)
+    sent = [depth_forward(density_one, density_two, forward_table(0, zero), rows_shape)]
+    sent[0], anchor = lax.optimization_barrier((sent[0], zero))
+    for chunk in range(1, chunks):
+        sent.append(depth_forward(density_one, density_two, forward_table(chunk, anchor), rows_shape))
+    tables = plane_tables(anchor, grid_x, grid_y, count_y)
+    back_table = inverse_table(anchor)
+    back = []
+    for chunk in range(chunks):
+        moved = lax.all_to_all(sent[chunk], ("gx", "gy"), split_axis=0, concat_axis=0, tiled=True)
+        lines = planes(moved, tables, count_x, count_y, 1.0 / cell_total)
+        back.append(lax.all_to_all(lines, ("gx", "gy"), split_axis=0, concat_axis=0, tiled=True))
+    return depth_inverse(back, back_table)
+
+
 def solution(mesh):
     return jax.shard_map(
         on_device,

time: 2130 us -> 1180 us (0.55)
  matrix products: 775 us -> 0 us
  Pallas kernels: 0 us -> 263 us
  waiting for transfers between devices: 1070 us -> 825 us
  local copies, waits for them, and re-layouts: 157 us -> 0 us
  other arithmetic: 110 us -> 72.2 us
    dot_general x9 -> x0, matrix products: 775 us -> none  [the longest x1 433 us: on_device(): jnp.einsum('fdspkjy,psyrq->fdrkjq', moved, y_forward, precision=exact_mode)]
    pallas_call x0 -> x5, Pallas kernels: none -> 263 us  [the longest x2 171 us: planes(): pl.pallas_call(body, grid=(kz_chunk,), in_specs=[pl.BlockSpec((devices, 2...]
    all_to_all x2 -> x4, waiting for transfers between devices: 1070 us -> 825 us  [the longest x2 547 us: on_device(): lax.all_to_all(sent[chunk], ('gx', 'gy'), split_axis=0, concat_axis=0, ti...]
    reshape x2 -> x0, local copies, waits for them, and re-layouts: 80.5 us -> none  [the longest x1 52.6 us: on_device(): moved = moved.reshape(2, count_x, count_y, 2, kz_slices, x_local, y_local)]
    convert_element_type x0 -> x5, other arithmetic: none -> 72 us  [cosine_pair(): return (high.astype(jnp.bfloat16), (turned - high).astype(jnp.bfloat16))]
    transpose x2 -> x0, local copies, waits for them, and re-layouts: 62.3 us -> none  [the longest x1 39.3 us: on_device(): jnp.einsum('fdspkjy,psyrq->fdrkjq', moved, y_forward, precision=exact_mode)]
    another operation x5 -> x0, other arithmetic: 43.1 us -> none  [the longest x1 23 us: on_device(): jnp.stack([real_part * forward_cos + imag_part * forward_sin, imag_part *...]
    add x3 -> x5, other arithmetic: 27.3 us -> 0.04 us  [the longest x1 0.01 us: plane_tables(): inner_y = inner // (2 * y_local) * y_local + inner % y_local]
  transfers between devices with their start and end apart: 2 -> 4, of which waited for: 2 -> 4; matrix products, arithmetic and copies ran while one was open for 1% -> 6% of each run, Pallas kernels for 0% -> 17%
where the time goes in v1:
time: 1180 us
  waiting for transfers between devices  825 us (70%)
  Pallas kernels  263 us (22%)
  other arithmetic  72.2 us (6%)
  starting transfers between devices  19.1 us (2%)
    all_to_all x2, waiting for transfers between devices, on_device(): lax.all_to_all(sent[chunk], ('gx', 'gy'), split_axis=0, concat_axis=0, ti...  547 us
    all_to_all x2, waiting for transfers between devices, on_device(): lax.all_to_all(lines, ('gx', 'gy'), split_axis=0, concat_axis=0, tiled=True)  278 us
    pallas_call x2, Pallas kernels, planes(): pl.pallas_call(body, grid=(kz_chunk,), in_specs=[pl.BlockSpec((devices, 2...  171 us
    convert_element_type x5, other arithmetic, cosine_pair(): return (high.astype(jnp.bfloat16), (turned - high).astype(jnp.bfloat16))  72 us
    pallas_call x2, Pallas kernels, depth_forward(): pl.pallas_call(depth_forward_kernel, grid=(y_local // Y_BLOCK,), in_specs...  65.9 us
    pallas_call x1, Pallas kernels, depth_inverse(): pl.pallas_call(depth_inverse_kernel, grid=(y_local // Y_BLOCK,), in_specs...  26.5 us
  transfers between devices with their start and end apart: 4, of which 4 were waited for; matrix products, arithmetic and copies ran while one was open for 6% of the time, Pallas kernels for 17%

profile of v1, /device:TPU:0, one launch (start us, length us, event | category | flops | bytes accessed | tf_op | source)
XLA Modules:
  0.0 1179.6 jit_solution(6125292527439241965)
XLA Ops:
  0.0 2.8 fusion.26
  2.8 32.9 %depth_forward.2 = f32[32,2,2,4,64,128]{5,4,3,2,1,0:T(8,128)} custom-call(f32[128,64,512]{2,1,0:T(8,128)} %one_ref.3, f32[128,64,512]{2,1,0:T(8,128)} %two_ref.3, bf16[512,256]{1,0:T(8,128)(2,1)} %get-tuple-element.26.high_ref, bf16[512,256]{1,0:T(8,128)(2,1)} %get-tuple-element.25.low_ref), custom_call_target="tpu_custom_call" | custom-call | tf_op jit(solution)/shard_map/depth_forward/pallas_call | solution.py:199
  35.7 7.5 all-to-all-start
  43.2 2.8 fusion.27
  46.0 33.0 %depth_forward.3 = f32[32,2,2,4,64,128]{5,4,3,2,1,0:T(8,128)} custom-call(f32[128,64,512]{2,1,0:T(8,128)} %one_ref.3, f32[128,64,512]{2,1,0:T(8,128)} %two_ref.3, bf16[512,256]{1,0:T(8,128)(2,1)} %get-tuple-element.24.high_ref, bf16[512,256]{1,0:T(8,128)(2,1)} %get-tuple-element.23.low_ref), custom_call_target="tpu_custom_call" | custom-call | tf_op jit(solution)/shard_map/depth_forward/pallas_call | solution.py:199
  78.9 328.8 %all-to-all-done.refs_0_ = f32[32,2,2,4,64,128]{5,4,3,2,1,0:T(8,128)} async-done(((f32[32,2,2,4,64,128]{5,4,3,2,1,0:T(8,128)}), f32[32,2,2,4,64,128]{5,4,3,2,1,0:T(8,128)}, u32[]{:S(2)}, u32[]{:S(2)}) %all-to-all-start) | async-done | bytes 16777248 | tf_op jit(solution)/shard_map/all_to_all | solution.py:434
  407.7 4.1 all-to-all-start.2
  411.9 9.3 fusion.15
  421.2 51.8 %fusion.2 = (bf16[1024,1024]{1,0:T(8,128)(2,1)}, bf16[1024,1024]{1,0:T(8,128)(2,1)}, bf16[1024,1024]{1,0:T(8,128)(2,1)}, bf16[1024,1024]{1,0:T(8,128)(2,1)}, bf1...) fusion(s32[1024]{0:T(1024)S(1)} %add_select_fusion.8, s32[1024]{0:T(1024)S(1)} %add_select_fusion.15, ...), kind=kLoop, calls=%fused_computation.17 | loop fusion | flops 69206016 | bytes 12607488 | tf_op jit(solution)/shard_map/convert_element_type | solution.py:153
  473.0 85.4 %planes.2 = f32[32,2,4,64,128]{4,3,2,1,0:T(8,128)} custom-call(f32[32,2,2,4,64,128]{5,4,3,2,1,0:T(8,128)} %all-to-all-done.refs_0_, bf16[1024,1024]{1,0:T(8,128)(2,1)} %get-tuple-element.19.refs_1_, bf16[1024,1024]{1,0:T(8,128)(2,1)} %get-tuple-element.20.refs_2_, bf16[1024,1024]{1,0:T(8,128)(2,1)} %get-tuple-element.17.refs_3_, ...), custom_call_target="tpu_custom_call" | custom-call | tf_op jit(solution)/shard_map/planes/pallas_call | solution.py:348
  558.4 217.7 %all-to-all-done.2.refs_0_ = f32[32,2,2,4,64,128]{5,4,3,2,1,0:T(8,128)} async-done(((f32[32,2,2,4,64,128]{5,4,3,2,1,0:T(8,128)}), f32[32,2,2,4,64,128]{5,4,3,2,1,0:T(8,128)}, u32[]{:S(2)}, u32[]{:S(2)}) %all-to-all-start.2) | async-done | bytes 16777248 | tf_op jit(solution)/shard_map/all_to_all | solution.py:434
  776.2 3.9 all-to-all-start.1
  780.1 85.5 %planes.3 = f32[32,2,4,64,128]{4,3,2,1,0:T(8,128)} custom-call(f32[32,2,2,4,64,128]{5,4,3,2,1,0:T(8,128)} %all-to-all-done.2.refs_0_, bf16[1024,1024]{1,0:T(8,128)(2,1)} %get-tuple-element.19.refs_1_, bf16[1024,1024]{1,0:T(8,128)(2,1)} %get-tuple-element.20.refs_2_, bf16[1024,1024]{1,0:T(8,128)(2,1)} %get-tuple-element.17.refs_3_, ...), custom_call_target="tpu_custom_call" | custom-call | tf_op jit(solution)/shard_map/planes/pallas_call | solution.py:348
  865.5 99.1 %all-to-all-done.1.refs_0_ = f32[32,2,4,64,128]{4,3,2,1,0:T(8,128)} async-done(((f32[32,2,4,64,128]{4,3,2,1,0:T(8,128)}), f32[32,2,4,64,128]{4,3,2,1,0:T(8,128)}, u32[]{:S(2)}, u32[]{:S(2)}) %all-to-all-start.1) | async-done | bytes 8388640 | tf_op jit(solution)/shard_map/all_to_all | solution.py:436
  964.6 3.7 all-to-all-start.3
  968.4 5.4 fusion.20
  973.8 179.3 %all-to-all-done.3.refs_1_ = f32[32,2,4,64,128]{4,3,2,1,0:T(8,128)} async-done(((f32[32,2,4,64,128]{4,3,2,1,0:T(8,128)}), f32[32,2,4,64,128]{4,3,2,1,0:T(8,128)}, u32[]{:S(2)}, u32[]{:S(2)}) %all-to-all-start.3) | async-done | bytes 8388640 | tf_op jit(solution)/shard_map/all_to_all | solution.py:436
  1153.1 26.5 %depth_inverse.1 = f32[128,64,512]{2,1,0:T(8,128)} custom-call(f32[32,2,4,64,128]{4,3,2,1,0:T(8,128)} %all-to-all-done.1.refs_0_, f32[32,2,4,64,128]{4,3,2,1,0:T(8,128)} %all-to-all-done.3.refs_1_, bf16[512,512]{1,0:T(8,128)(2,1)} %get-tuple-element.22.refs_2_, bf16[512,512]{1,0:T(8,128)(2,1)} %get-tuple-element.21.refs_3_), custom_call_target="tpu_custom_call" | custom-call | tf_op jit(solution)/shard_map/depth_inverse/pallas_call | solution.py:242
  (14 shorter events, 0.1 us)
Async XLA Ops:
  35.7 372.0 %all-to-all-start = ((f32[32,2,2,4,64,128]{5,4,3,2,1,0:T(8,128)}), f32[32,2,2,4,64,128]{5,4,3,2,1,0:T(8,128)}, u32[]{:S(2)}, u32[]{:S(2)}) async-start(f32[32,2,2,4,64,128]{5,4,3,2,1,0:T(8,128)} %depth_forward.2), calls=%async_computation | async-start | bytes 33554432 | tf_op jit(solution)/shard_map/all_to_all | solution.py:434
  407.7 368.4 %all-to-all-start.2 = ((f32[32,2,2,4,64,128]{5,4,3,2,1,0:T(8,128)}), f32[32,2,2,4,64,128]{5,4,3,2,1,0:T(8,128)}, u32[]{:S(2)}, u32[]{:S(2)}) async-start(f32[32,2,2,4,64,128]{5,4,3,2,1,0:T(8,128)} %depth_forward.3), calls=%async_computation.2 | async-start | bytes 33554432 | tf_op jit(solution)/shard_map/all_to_all | solution.py:434
  776.2 188.5 %all-to-all-start.1 = ((f32[32,2,4,64,128]{4,3,2,1,0:T(8,128)}), f32[32,2,4,64,128]{4,3,2,1,0:T(8,128)}, u32[]{:S(2)}, u32[]{:S(2)}) async-start(f32[32,2,4,64,128]{4,3,2,1,0:T(8,128)} %planes.2), calls=%async_computation.1 | async-start | bytes 16777216 | tf_op jit(solution)/shard_map/all_to_all | solution.py:436
  964.6 188.5 %all-to-all-start.3 = ((f32[32,2,4,64,128]{4,3,2,1,0:T(8,128)}), f32[32,2,4,64,128]{4,3,2,1,0:T(8,128)}, u32[]{:S(2)}, u32[]{:S(2)}) async-start(f32[32,2,4,64,128]{4,3,2,1,0:T(8,128)} %planes.3), calls=%async_computation.3 | async-start | bytes 16777216 | tf_op jit(solution)/shard_map/all_to_all | solution.py:436

commit v2 on v1

--- a/solution.py
+++ b/solution.py
@@ -128,7 +128,6 @@
 
 
 VMEM_LIMIT = 60 * 1024 * 1024
-MAX_CHUNKS = 2
 Y_BLOCK = 8
 
 
@@ -153,102 +152,93 @@
     return high.astype(jnp.bfloat16), (turned - high).astype(jnp.bfloat16)
 
 
-def depth_rows(chunk, chunks, devices, kz_slices):
-    per_chunk = kz_slices // chunks
+def depth_rows(chunk, devices, kz_slices):
+    per_chunk = kz_slices // 2
     rows = jnp.arange(devices * 2 * per_chunk, dtype=jnp.int32)
     device = rows // (2 * per_chunk)
     flag = rows // per_chunk % 2
-    return device * kz_slices + chunk * per_chunk + rows % per_chunk, flag
-
-
-def depth_forward_kernel(one_ref, two_ref, high_ref, low_ref, out_ref, turn_ref):
+    return device * kz_slices + rows % per_chunk * 2 + chunk, flag
+
+
+def depth_forward_kernel(one_ref, two_ref, high_ref, low_ref, out_ref, *turn_refs, sign):
     x_local, y_block, depth = one_ref.shape
     rows = high_ref.shape[1]
     lines = x_local * y_block
-    step = min(256, lines)
     group = out_ref.shape[2] * out_ref.shape[3]
     flat_out = out_ref.reshape(2 * rows * y_block, x_local)
     for field, ref in enumerate((one_ref, two_ref)):
         flat = ref.reshape(lines, depth)
-
-        def multiply(i, carry):
-            high, low = split(flat[pl.ds(i * step, step), :])
-            product = dot3(high, low, high_ref[...], low_ref[...])
-            for part in range(rows // 128):
-                turn_ref[field, part, pl.ds(i * step, step), :] = product[:, part * 128 : part * 128 + 128]
-            return carry
-
-        lax.fori_loop(0, lines // step, multiply, 0)
-    for field in range(2):
+        near, far = flat[:, : depth // 2], flat[:, depth // 2 :]
+        high, low = split(near + far if sign > 0 else near - far)
+        product = dot3(high, low, high_ref[...], low_ref[...])
         for part in range(rows // 128):
-            lanes = turn_ref.at[field, part]
+            lanes = turn_refs[field * (rows // 128) + part]
+            lanes[...] = product[:, part * 128 : part * 128 + 128]
             for j in range(y_block):
-                block = lanes[pl.ds(j, x_local, stride=y_block), :]
-                turned = block.T
+                turned = lanes[pl.ds(j, x_local, stride=y_block), :].T
                 for d in range(128 // group):
                     start = (2 * (part * (128 // group) + d) + field) * group * y_block + j
                     flat_out[pl.ds(start, group, stride=y_block), :] = turned[d * group : d * group + group]
 
 
-def depth_forward(one, two, table, rows_shape):
+def depth_forward(one, two, table, rows_shape, sign):
     x_local, y_local, depth = one.shape
     rows = math.prod(rows_shape)
     out_rows = (rows_shape[0], 2, *rows_shape[1:])
     field_spec = pl.BlockSpec((x_local, Y_BLOCK, depth), lambda i: (0, i, 0))
-    table_spec = pl.BlockSpec((depth, rows), lambda i: (0, 0))
+    table_spec = pl.BlockSpec((depth // 2, rows), lambda i: (0, 0))
+
+    def body(*refs):
+        depth_forward_kernel(*refs, sign=sign)
+
     return pl.pallas_call(
-        depth_forward_kernel,
+        body,
         grid=(y_local // Y_BLOCK,),
         in_specs=[field_spec, field_spec, table_spec, table_spec],
         out_specs=pl.BlockSpec((*out_rows, Y_BLOCK, x_local), lambda i: (0, 0, 0, 0, i, 0)),
         out_shape=jax.ShapeDtypeStruct((*out_rows, y_local, x_local), jnp.float32),
-        scratch_shapes=[pltpu.VMEM((2, rows // 128, x_local * Y_BLOCK, 128), jnp.float32)],
+        scratch_shapes=[pltpu.VMEM((x_local * Y_BLOCK, 128), jnp.float32)] * (2 * rows // 128),
         compiler_params=pltpu.CompilerParams(vmem_limit_bytes=VMEM_LIMIT),
         name="depth_forward",
     )(one, two, *table)
 
 
-def depth_inverse_kernel(*refs):
-    *part_refs, high_ref, low_ref, out_ref, turn_ref = refs
+def depth_inverse_kernel(even_ref, odd_ref, even_high, even_low, odd_high, odd_low, out_ref, *turn_refs):
     x_local, y_block, depth = out_ref.shape
     lines = x_local * y_block
-    blocks = 0
-    for part_ref in part_refs:
-        rows = part_ref.shape[0] * part_ref.shape[1] * part_ref.shape[2]
+    rows = even_high.shape[0]
+    sums = []
+    for p, (part_ref, high_ref, low_ref) in enumerate(
+        ((even_ref, even_high, even_low), (odd_ref, odd_high, odd_low))
+    ):
         flat = part_ref.reshape(rows * y_block, x_local)
-        for part in range(rows // 128):
+        turns = turn_refs[p * (rows // 128) : (p + 1) * (rows // 128)]
+        for part, turn in enumerate(turns):
             for j in range(y_block):
                 block = flat[pl.ds(part * 128 * y_block + j, 128, stride=y_block), :]
-                turn_ref[blocks, pl.ds(j, x_local, stride=y_block), :] = block.T
-            blocks += 1
-    step = min(256, lines)
+                turn[pl.ds(j, x_local, stride=y_block), :] = block.T
+        high, low = split(jnp.concatenate([turn[...] for turn in turns], axis=1))
+        sums.append(dot3(high, low, high_ref[...], low_ref[...]))
     flat_out = out_ref.reshape(lines, depth)
-
-    def multiply(i, carry):
-        window = pl.ds(i * step, step)
-        left = jnp.concatenate([turn_ref[b, window, :] for b in range(blocks)], axis=1)
-        high, low = split(left)
-        flat_out[window, :] = dot3(high, low, high_ref[...], low_ref[...])
-        return carry
-
-    lax.fori_loop(0, lines // step, multiply, 0)
-
-
-def depth_inverse(parts, table):
+    flat_out[:, : depth // 2] = sums[0] + sums[1]
+    flat_out[:, depth // 2 :] = sums[0] - sums[1]
+
+
+def depth_inverse(parts, tables):
     devices, two, kz_chunk, y_local, x_local = parts[0].shape
-    rows, depth = table[0].shape
+    rows, half = tables[0][0].shape
     part_spec = pl.BlockSpec((devices, two, kz_chunk, Y_BLOCK, x_local), lambda i: (0, 0, 0, i, 0))
-    table_spec = pl.BlockSpec((rows, depth), lambda i: (0, 0))
+    table_spec = pl.BlockSpec((rows, half), lambda i: (0, 0))
     return pl.pallas_call(
         depth_inverse_kernel,
         grid=(y_local // Y_BLOCK,),
-        in_specs=[part_spec] * len(parts) + [table_spec, table_spec],
-        out_specs=pl.BlockSpec((x_local, Y_BLOCK, depth), lambda i: (0, i, 0)),
-        out_shape=jax.ShapeDtypeStruct((x_local, y_local, depth), jnp.float32),
-        scratch_shapes=[pltpu.VMEM((rows // 128, x_local * Y_BLOCK, 128), jnp.float32)],
+        in_specs=[part_spec] * 2 + [table_spec] * 4,
+        out_specs=pl.BlockSpec((x_local, Y_BLOCK, 2 * half), lambda i: (0, i, 0)),
+        out_shape=jax.ShapeDtypeStruct((x_local, y_local, 2 * half), jnp.float32),
+        scratch_shapes=[pltpu.VMEM((x_local * Y_BLOCK, 128), jnp.float32)] * (2 * rows // 128),
         compiler_params=pltpu.CompilerParams(vmem_limit_bytes=VMEM_LIMIT),
         name="depth_inverse",
-    )(*parts, *table)
+    )(*parts, *tables[0], *tables[1])
 
 
 def plane_kernel(
@@ -400,41 +390,39 @@
     grid_x, grid_y = x_local * count_x, y_local * count_y
     devices = count_x * count_y
     kz_slices = depth // 2 // devices
-    chunks = MAX_CHUNKS if kz_slices % MAX_CHUNKS == 0 else 1
-    kz_chunk = kz_slices // chunks
+    kz_chunk = kz_slices // 2
     rows = devices * 2 * kz_chunk
-    fits = x_local % 128 == 0 and y_local % 8 == 0 and rows % 128 == 0 and 2 * kz_chunk % 8 == 0 and grid_x % 256 == 0 and grid_y % 256 == 0
+    fits = x_local % 128 == 0 and y_local % 8 == 0 and grid_x % 256 == 0 and grid_y % 256 == 0
+    fits = fits and kz_slices % 8 == 0 and rows % 128 == 0 and depth % 256 == 0
     if not fits:
         return generic_device(density_one, density_two)
     cell_total = float(grid_x * grid_y * depth)
-    cells = jnp.arange(depth, dtype=jnp.int32)
+    cells = jnp.arange(depth // 2, dtype=jnp.int32)
     rows_shape = (devices, 2, kz_chunk)
 
     def forward_table(chunk, anchor):
-        wave, flag = depth_rows(chunk, chunks, devices, kz_slices)
+        wave, flag = depth_rows(chunk, devices, kz_slices)
         wave = wave + anchor
         return cosine_pair(cells[:, None] * wave[None, :] + flag[None, :] * (depth // 4), depth)
 
-    def inverse_table(anchor):
-        waves, flags = zip(*(depth_rows(chunk, chunks, devices, kz_slices) for chunk in range(chunks)))
-        wave = jnp.concatenate(waves) + anchor
-        flag = jnp.concatenate(flags)
+    def inverse_table(chunk, anchor):
+        wave, flag = depth_rows(chunk, devices, kz_slices)
+        wave = wave + anchor
         weight = jnp.where(wave == 0, 1.0, 2.0) * (1.0 / math.sqrt(cell_total))
         return cosine_pair(wave[:, None] * cells[None, :] + flag[:, None] * (depth // 4), depth, weight[:, None])
 
     zero = jnp.zeros((), jnp.int32)
-    sent = [depth_forward(density_one, density_two, forward_table(0, zero), rows_shape)]
-    sent[0], anchor = lax.optimization_barrier((sent[0], zero))
-    for chunk in range(1, chunks):
-        sent.append(depth_forward(density_one, density_two, forward_table(chunk, anchor), rows_shape))
+    even = depth_forward(density_one, density_two, forward_table(0, zero), rows_shape, 1)
+    even, anchor = lax.optimization_barrier((even, zero))
+    odd = depth_forward(density_one, density_two, forward_table(1, anchor), rows_shape, -1)
     tables = plane_tables(anchor, grid_x, grid_y, count_y)
-    back_table = inverse_table(anchor)
+    back_tables = [inverse_table(chunk, anchor) for chunk in range(2)]
     back = []
-    for chunk in range(chunks):
-        moved = lax.all_to_all(sent[chunk], ("gx", "gy"), split_axis=0, concat_axis=0, tiled=True)
+    for sent in (even, odd):
+        moved = lax.all_to_all(sent, ("gx", "gy"), split_axis=0, concat_axis=0, tiled=True)
         lines = planes(moved, tables, count_x, count_y, 1.0 / cell_total)
         back.append(lax.all_to_all(lines, ("gx", "gy"), split_axis=0, concat_axis=0, tiled=True))
-    return depth_inverse(back, back_table)
+    return depth_inverse(back, back_tables)
 
 
 def solution(mesh):

time: 1180 us -> 1160 us (0.983)
  blocking collectives: 0 us -> 188 us
  waiting for transfers between devices: 825 us -> 654 us
  Pallas kernels: 263 us -> 236 us
    all_to_all x0 -> x1, blocking collectives: none -> 188 us  [on_device(): lax.all_to_all(lines, ('gx', 'gy'), split_axis=0, concat_axis=0, tiled=True)]
    all_to_all x2 -> x1, waiting for transfers between devices: 278 us -> 99.1 us  [on_device(): lax.all_to_all(lines, ('gx', 'gy'), split_axis=0, concat_axis=0, tiled=True)]
    pallas_call x2, Pallas kernels: 65.9 us -> 45.6 us  [depth_forward(): pl.pallas_call(body, grid=(y_local // Y_BLOCK,), in_specs=[field_spec, fi...]
    convert_element_type x5 -> x4, other arithmetic: 72 us -> 66.9 us  [cosine_pair(): return (high.astype(jnp.bfloat16), (turned - high).astype(jnp.bfloat16))]
  transfers between devices with their start and end apart: 4 -> 3, of which waited for: 4 -> 3; matrix products, arithmetic and copies ran while one was open for 6% -> 6% of each run, Pallas kernels for 17% -> 17%
where the time goes in v2:
time: 1160 us
  waiting for transfers between devices  654 us (56%)
  Pallas kernels  236 us (20%)
  blocking collectives  188 us (16%)
  other arithmetic  67.1 us (6%)
  starting transfers between devices  15.4 us (1%)
    all_to_all x2, waiting for transfers between devices, on_device(): lax.all_to_all(sent, ('gx', 'gy'), split_axis=0, concat_axis=0, tiled=True)  555 us
    all_to_all x1, blocking collectives, on_device(): lax.all_to_all(lines, ('gx', 'gy'), split_axis=0, concat_axis=0, tiled=True)  188 us
    pallas_call x2, Pallas kernels, planes(): pl.pallas_call(body, grid=(kz_chunk,), in_specs=[pl.BlockSpec((devices, 2...  171 us
    all_to_all x1, waiting for transfers between devices, on_device(): lax.all_to_all(lines, ('gx', 'gy'), split_axis=0, concat_axis=0, tiled=True)  99.1 us
    convert_element_type x4, other arithmetic, cosine_pair(): return (high.astype(jnp.bfloat16), (turned - high).astype(jnp.bfloat16))  66.9 us
    pallas_call x2, Pallas kernels, depth_forward(): pl.pallas_call(body, grid=(y_local // Y_BLOCK,), in_specs=[field_spec, fi...  45.6 us
  transfers between devices with their start and end apart: 3, of which 3 were waited for; matrix products, arithmetic and copies ran while one was open for 6% of the time, Pallas kernels for 17%

profile of v2, /device:TPU:0, one launch (start us, length us, event | category | flops | bytes accessed | tf_op | source)
XLA Modules:
  0.0 1160.9 jit_solution(16077199936204070266)
XLA Ops:
  0.0 1.7 fusion.20
  1.7 22.8 %depth_forward.2 = f32[32,2,2,4,64,128]{5,4,3,2,1,0:T(8,128)} custom-call(f32[128,64,512]{2,1,0:T(8,128)} %refs_0_.3, f32[128,64,512]{2,1,0:T(8,128)} %refs_1_.3, bf16[256,256]{1,0:T(8,128)(2,1)} %get-tuple-element.26.refs_2_, bf16[256,256]{1,0:T(8,128)(2,1)} %get-tuple-element.25.refs_3_), custom_call_target="tpu_custom_call" | custom-call | tf_op jit(solution)/shard_map/depth_forward/pallas_call | solution.py:194
  24.5 7.4 all-to-all-start
  32.0 4.2 fusion.23
  36.2 22.8 %depth_forward.3 = f32[32,2,2,4,64,128]{5,4,3,2,1,0:T(8,128)} custom-call(f32[128,64,512]{2,1,0:T(8,128)} %refs_0_.3, f32[128,64,512]{2,1,0:T(8,128)} %refs_1_.3, bf16[256,256]{1,0:T(8,128)(2,1)} %get-tuple-element.23.refs_2_, bf16[256,256]{1,0:T(8,128)(2,1)} %get-tuple-element.24.refs_3_), custom_call_target="tpu_custom_call" | custom-call | tf_op jit(solution)/shard_map/depth_forward/pallas_call | solution.py:194
  59.0 337.5 %all-to-all-done.refs_0_ = f32[32,2,2,4,64,128]{5,4,3,2,1,0:T(8,128)} async-done(((f32[32,2,2,4,64,128]{5,4,3,2,1,0:T(8,128)}), f32[32,2,2,4,64,128]{5,4,3,2,1,0:T(8,128)}, u32[]{:S(2)}, u32[]{:S(2)}) %all-to-all-start) | async-done | bytes 16777248 | tf_op jit(solution)/shard_map/all_to_all | solution.py:422
  396.5 4.1 all-to-all-start.2
  400.7 9.3 fusion.15
  410.0 51.7 %fusion.2 = (bf16[1024,1024]{1,0:T(8,128)(2,1)}, bf16[1024,1024]{1,0:T(8,128)(2,1)}, bf16[1024,1024]{1,0:T(8,128)(2,1)}, bf16[1024,1024]{1,0:T(8,128)(2,1)}, bf1...) fusion(s32[1024]{0:T(1024)S(1)} %add_select_fusion.9, s32[1024]{0:T(1024)S(1)} %add_select_fusion.16, ...), kind=kLoop, calls=%fused_computation.17 | loop fusion | flops 69206016 | bytes 12607488 | tf_op jit(solution)/shard_map/convert_element_type | solution.py:152
  461.8 85.4 %planes.2 = f32[32,2,4,64,128]{4,3,2,1,0:T(8,128)} custom-call(f32[32,2,2,4,64,128]{5,4,3,2,1,0:T(8,128)} %all-to-all-done.refs_0_, bf16[1024,1024]{1,0:T(8,128)(2,1)} %get-tuple-element.17.refs_1_, bf16[1024,1024]{1,0:T(8,128)(2,1)} %get-tuple-element.18.refs_2_, bf16[1024,1024]{1,0:T(8,128)(2,1)} %get-tuple-element.15.refs_3_, ...), custom_call_target="tpu_custom_call" | custom-call | tf_op jit(solution)/shard_map/planes/pallas_call | solution.py:338
  547.2 217.8 %all-to-all-done.2.refs_0_ = f32[32,2,2,4,64,128]{5,4,3,2,1,0:T(8,128)} async-done(((f32[32,2,2,4,64,128]{5,4,3,2,1,0:T(8,128)}), f32[32,2,2,4,64,128]{5,4,3,2,1,0:T(8,128)}, u32[]{:S(2)}, u32[]{:S(2)}) %all-to-all-start.2) | async-done | bytes 16777248 | tf_op jit(solution)/shard_map/all_to_all | solution.py:422
  765.0 3.9 all-to-all-start.1
  768.9 85.5 %planes.3 = f32[32,2,4,64,128]{4,3,2,1,0:T(8,128)} custom-call(f32[32,2,2,4,64,128]{5,4,3,2,1,0:T(8,128)} %all-to-all-done.2.refs_0_, bf16[1024,1024]{1,0:T(8,128)(2,1)} %get-tuple-element.17.refs_1_, bf16[1024,1024]{1,0:T(8,128)(2,1)} %get-tuple-element.18.refs_2_, bf16[1024,1024]{1,0:T(8,128)(2,1)} %get-tuple-element.15.refs_3_, ...), custom_call_target="tpu_custom_call" | custom-call | tf_op jit(solution)/shard_map/planes/pallas_call | solution.py:338
  854.4 99.1 %all-to-all-done.1.even_ref = f32[32,2,4,64,128]{4,3,2,1,0:T(8,128)} async-done(((f32[32,2,4,64,128]{4,3,2,1,0:T(8,128)}), f32[32,2,4,64,128]{4,3,2,1,0:T(8,128)}, u32[]{:S(2)}, u32[]{:S(2)}) %all-to-all-start.1) | async-done | bytes 8388640 | tf_op jit(solution)/shard_map/all_to_all | solution.py:424
  953.4 188.4 %all_to_all.20.odd_ref = f32[32,2,4,64,128]{4,3,2,1,0:T(8,128)} all-to-all(f32[32,2,4,64,128]{4,3,2,1,0:T(8,128)} %planes.3), channel_id=1, replica_groups=mesh['gx'=4,'gy'=8] {'gx','gy'}, dimensions={0} | all-to-all | bytes 16777216 | tf_op jit(solution)/shard_map/all_to_all | solution.py:424
  1141.9 19.0 %depth_inverse.1 = f32[128,64,512]{2,1,0:T(8,128)} custom-call(f32[32,2,4,64,128]{4,3,2,1,0:T(8,128)} %all-to-all-done.1.even_ref, f32[32,2,4,64,128]{4,3,2,1,0:T(8,128)} %all_to_all.20.odd_ref, bf16[256,256]{1,0:T(8,128)(2,1)} %get-tuple-element.27.even_high, bf16[256,256]{1,0:T(8,128)(2,1)} %get-tuple-element.28.even_low, ...), custom_call_target="tpu_custom_call" | custom-call | tf_op jit(solution)/shard_map/depth_inverse/pallas_call | solution.py:232
  (13 shorter events, 0.1 us)
Async XLA Ops:
  24.5 372.0 %all-to-all-start = ((f32[32,2,2,4,64,128]{5,4,3,2,1,0:T(8,128)}), f32[32,2,2,4,64,128]{5,4,3,2,1,0:T(8,128)}, u32[]{:S(2)}, u32[]{:S(2)}) async-start(f32[32,2,2,4,64,128]{5,4,3,2,1,0:T(8,128)} %depth_forward.2), calls=%async_computation | async-start | bytes 33554432 | tf_op jit(solution)/shard_map/all_to_all | solution.py:422
  396.5 368.5 %all-to-all-start.2 = ((f32[32,2,2,4,64,128]{5,4,3,2,1,0:T(8,128)}), f32[32,2,2,4,64,128]{5,4,3,2,1,0:T(8,128)}, u32[]{:S(2)}, u32[]{:S(2)}) async-start(f32[32,2,2,4,64,128]{5,4,3,2,1,0:T(8,128)} %depth_forward.3), calls=%async_computation.2 | async-start | bytes 33554432 | tf_op jit(solution)/shard_map/all_to_all | solution.py:422
  765.0 188.5 %all-to-all-start.1 = ((f32[32,2,4,64,128]{4,3,2,1,0:T(8,128)}), f32[32,2,4,64,128]{4,3,2,1,0:T(8,128)}, u32[]{:S(2)}, u32[]{:S(2)}) async-start(f32[32,2,4,64,128]{4,3,2,1,0:T(8,128)} %planes.2), calls=%async_computation.1 | async-start | bytes 16777216 | tf_op jit(solution)/shard_map/all_to_all | solution.py:424
